TPU v7x, 32 devices: a whole 2x2x4 slice. The times are simulated.
32 devices in a mesh: dp: 4 (over x, core), wide: 8 (over z, y).
Axes of the slice: x: 2, y: 2, z: 4, core: 2. Of those that a mesh axis runs over, the one named last changes fastest.
Arguments:
- streams: float32 [4, 4096, 2048], P(None, 'dp', 'wide'), may hold values from -8 to 8
- cotangent: float32 [4, 4096, 2048], P(None, 'dp', 'wide'), may hold values from -6 to 6
- w_query: bfloat16 [2048, 2048], P('dp', 'wide'), may hold values from -2 to 2
- w_key: bfloat16 [2048, 2048], P('dp', 'wide'), may hold values from -0.125 to 0.125
- w_value: bfloat16 [2048, 2048], P('dp', 'wide'), may hold values from -0.125 to 0.125
- w_out: bfloat16 [2048, 2048], P('wide', 'dp'), may hold values from -1 to 1
- w_gate: bfloat16 [2048, 8192], P('dp', 'wide'), may hold values from -0.125 to 0.125
- w_up: bfloat16 [2048, 8192], P('dp', 'wide'), may hold values from -0.125 to 0.125
- w_down: bfloat16 [8192, 2048], P('wide', 'dp'), may hold values from -0.0625 to 0.0625
- hyper: float32 [2, 4, 6], replicated, may hold values from 0.1 to 0.6
- doc_ids: int32 [4, 1024], P('dp'), may hold values from 0 to 3, never falling along the last dimension, each value on 1 to 512 neighbouring positions
- span_starts: int32 [4, 2], P('dp'), may hold values from 0 to 768, as said below
- span_lengths: int32 [4, 2], P('dp'), may hold values from 64 to 256
Outputs:
- out_streams: float32 [4, 4096, 2048], P(None, 'dp', 'wide')
- d_streams: float32 [4, 4096, 2048], P(None, 'dp', 'wide')
- grad_query: float32 [2048, 2048], P('dp', 'wide')
- grad_key: float32 [2048, 2048], P('dp', 'wide')
- grad_value: float32 [2048, 2048], P('dp', 'wide')
- grad_out: float32 [2048, 2048], P('wide', 'dp')
- grad_gate: float32 [2048, 8192], P('dp', 'wide')
- grad_up: float32 [2048, 8192], P('dp', 'wide')
- grad_down: float32 [8192, 2048], P('wide', 'dp')
- grad_hyper: float32 [2, 4, 6], replicated
- clip_scale: float32 [16], P('wide')
- query_clipped: float32 [2048, 2048], P('dp', 'wide')
- key_clipped: float32 [2048, 2048], P('dp', 'wide')
Inputs may be any that keep to these rules, and one draw needn't show every extreme that they name: `doc_ids`: each row's document numbers never fall; every document holds 1 to 512 tokens, and one holds exactly 512. `span_starts`: span k of a sequence starts and ends inside the k-th of 2 equal regions of the sequence.
All inputs are finite; a program needn't handle non-finite values.
Results may differ from a plain program's by a relative error of at most 0.018.
Values may be sent and summed in bfloat16 or wider, within the bound.
A program may use at most 192 MiB of HBM per device.

v0:
```python
import math
import jax
import jax.numpy as jnp
from jax import lax
from jax.sharding import PartitionSpec as P

D = 2048
H = 16
CLIP_TAU = 6
EPSILON = 1e-05
MASKED = -1e30


def rope_tables(length, head_size):
    half_size = head_size // 2
    inverse = 10000.0 ** (-2.0 * jnp.arange(half_size, dtype=jnp.float32) / head_size)
    angles = jnp.arange(length, dtype=jnp.float32)[:, None] * inverse[None, :]
    cosine_table = jnp.cos(angles)
    sine_table = jnp.sin(angles)
    return (
        jnp.concatenate([cosine_table, cosine_table], axis=1),
        jnp.concatenate([sine_table, sine_table], axis=1),
    )


def rotate(values, cosine_table, sine_table):
    half_size = values.shape[-1] // 2
    turned = jnp.concatenate([-values[..., half_size:], values[..., :half_size]], axis=-1)
    return values * cosine_table[:, None, :] + turned * sine_table[:, None, :]


def rotate_back(grads, cosine_table, sine_table):
    half_size = grads.shape[-1] // 2
    scaled = grads * sine_table[:, None, :]
    turned = jnp.concatenate([scaled[..., half_size:], -scaled[..., :half_size]], axis=-1)
    return grads * cosine_table[:, None, :] + turned


def mix_inputs(weights_in, stream_set):
    return jnp.sum(weights_in[:, None, None] * stream_set, axis=0)


def mix_streams(matrix, stream_set):
    return jnp.sum(matrix[:, :, None, None] * stream_set[None, :, :, :], axis=1)


def mix_back(matrix, grads):
    return jnp.sum(matrix[:, :, None, None] * grads[:, None, :, :], axis=0)


def hyper_rows(pre_grad, post_grad, mix_grad):
    return jnp.concatenate([pre_grad[:, None], post_grad[:, None], mix_grad], axis=1)


def span_labels(positions, starts, lengths):
    inside = (positions[:, None] >= starts[None, :]) & (
        positions[:, None] < (starts + lengths)[None, :]
    )
    numbers = jnp.arange(1, starts.shape[0] + 1, dtype=jnp.int32)
    return jnp.sum(jnp.where(inside, numbers[None, :], 0), axis=1)


def block_mask(doc_row, labels, start_row, count_rows):
    key_pos = jnp.arange(doc_row.shape[0], dtype=jnp.int32)
    query_pos = start_row + jnp.arange(count_rows, dtype=jnp.int32)
    query_docs = lax.dynamic_slice_in_dim(doc_row, start_row, count_rows)
    query_labels = lax.dynamic_slice_in_dim(labels, start_row, count_rows)
    same_doc = query_docs[:, None] == doc_row[None, :]
    causal = key_pos[None, :] <= query_pos[:, None]
    joint_span = (query_labels[:, None] > 0) & (query_labels[:, None] == labels[None, :])
    return same_doc & (causal | joint_span)


def attend_forward(queries, keys_roped, values, doc_row, starts, lengths, score_scale):
    length, head_count, head_size = queries.shape
    block_rows = min(512, length)
    labels = span_labels(jnp.arange(length, dtype=jnp.int32), starts, lengths)

    def one_block(block_index):
        start_row = block_index * block_rows
        query_rows = lax.dynamic_slice_in_dim(queries, start_row, block_rows, 0)
        scores = (
            jnp.einsum("qhd,khd->hqk", query_rows, keys_roped, preferred_element_type=jnp.float32)
            * score_scale
        )
        allowed = block_mask(doc_row, labels, start_row, block_rows)
        masked = jnp.where(allowed[None, :, :], scores, MASKED)
        largest = jnp.max(masked, axis=2)
        exponent = jnp.exp(masked - largest[:, :, None])
        totals = jnp.sum(exponent, axis=2)
        weights_low = (exponent / totals[:, :, None]).astype(jnp.bfloat16)
        attended = jnp.einsum(
            "hqk,khd->qhd", weights_low, values, preferred_element_type=jnp.float32
        )
        return (attended, largest + jnp.log(totals), jnp.max(largest, axis=1))

    attended, log_sums, block_tops = lax.map(
        one_block, jnp.arange(length // block_rows, dtype=jnp.int32)
    )
    return (attended.reshape(length, head_count, head_size), log_sums, jnp.max(block_tops, axis=0))


def attend_backward(
    queries, keys_roped, values, dout, log_sums, doc_row, starts, lengths, score_scale
):
    length, head_count, head_size = queries.shape
    block_rows = min(512, length)
    labels = span_labels(jnp.arange(length, dtype=jnp.int32), starts, lengths)

    def one_block(carry, inputs):
        key_grad, value_grad = carry
        block_index, log_rows = inputs
        start_row = block_index * block_rows
        query_rows = lax.dynamic_slice_in_dim(queries, start_row, block_rows, 0)
        dout_rows = lax.dynamic_slice_in_dim(dout, start_row, block_rows, 0)
        scores = (
            jnp.einsum("qhd,khd->hqk", query_rows, keys_roped, preferred_element_type=jnp.float32)
            * score_scale
        )
        allowed = block_mask(doc_row, labels, start_row, block_rows)
        masked = jnp.where(allowed[None, :, :], scores, MASKED)
        weights_full = jnp.where(allowed[None, :, :], jnp.exp(masked - log_rows[:, :, None]), 0.0)
        weight_grad = jnp.einsum(
            "qhd,khd->hqk", dout_rows, values, preferred_element_type=jnp.float32
        )
        centre = jnp.sum(weights_full * weight_grad, axis=2, keepdims=True)
        score_grad = (weights_full * (weight_grad - centre)).astype(jnp.bfloat16)
        query_grad = score_scale * jnp.einsum(
            "hqk,khd->qhd", score_grad, keys_roped, preferred_element_type=jnp.float32
        )
        key_grad = key_grad + score_scale * jnp.einsum(
            "hqk,qhd->khd", score_grad, query_rows, preferred_element_type=jnp.float32
        )
        value_grad = value_grad + jnp.einsum(
            "hqk,qhd->khd",
            weights_full.astype(jnp.bfloat16),
            dout_rows,
            preferred_element_type=jnp.float32,
        )
        return ((key_grad, value_grad), query_grad)

    empty_grad = jnp.zeros((length, head_count, head_size), jnp.float32)
    count_blocks = length // block_rows
    (key_grad, value_grad), query_grad = lax.scan(
        one_block, (empty_grad, empty_grad), (jnp.arange(count_blocks, dtype=jnp.int32), log_sums)
    )
    return (query_grad.reshape(length, head_count, head_size), key_grad, value_grad)


def row_sums(first_term, second_term):
    return lax.psum((jnp.sum(first_term, axis=1), jnp.sum(second_term, axis=1)), "wide")


def features(piece):
    return lax.all_gather(piece, "wide", axis=1, tiled=True)


def branch_rows(partial_value):
    return lax.psum_scatter(partial_value, "wide", scatter_dimension=1, tiled=True)


def norm_forward(hidden):
    local_width = hidden.shape[1]
    full_width = local_width * lax.axis_size("wide")
    row_total, squares = row_sums(hidden, hidden * hidden)
    centre = row_total / full_width
    spread = squares / full_width - centre * centre
    inverse = lax.rsqrt(spread + EPSILON)
    normed = (hidden - centre[:, None]) * inverse[:, None]
    return (features(normed.astype(jnp.bfloat16)), normed, inverse)


def norm_backward(partial_value, normed, inverse):
    full_width = partial_value.shape[1]
    grad_rows = lax.psum_scatter(partial_value, "wide", scatter_dimension=1, tiled=True)
    row_total, row_cross = row_sums(grad_rows, grad_rows * normed)
    return inverse[:, None] * (
        grad_rows - row_total[:, None] / full_width - normed * row_cross[:, None] / full_width
    )


def per_device(
    streams,
    cotangent,
    w_query,
    w_key,
    w_value,
    w_out,
    w_gate,
    w_up,
    w_down,
    hyper,
    doc_ids,
    span_starts,
    span_lengths,
):
    seq_count, length = doc_ids.shape
    tokens = streams.shape[1]
    head_size = D // H
    column_count = w_query.shape[1]
    head_count = column_count // head_size
    score_scale = 1.0 / math.sqrt(head_size)
    cosine_table, sine_table = rope_tables(length, head_size)
    shape_heads = (seq_count, length, head_count, head_size)
    attn_pre, attn_post, attn_mix = (hyper[0, :, 0], hyper[0, :, 1], hyper[0, :, 2:])
    ffn_pre, ffn_post, ffn_mix = (hyper[1, :, 0], hyper[1, :, 1], hyper[1, :, 2:])
    query_w, key_w, value_w, out_w = (
        lax.all_gather(w_query, "dp", axis=0, tiled=True),
        lax.all_gather(w_key, "dp", axis=0, tiled=True),
        lax.all_gather(w_value, "dp", axis=0, tiled=True),
        lax.all_gather(w_out, "dp", axis=1, tiled=True),
    )
    gate_w, up_w, down_w = (
        lax.all_gather(w_gate, "dp", axis=0, tiled=True),
        lax.all_gather(w_up, "dp", axis=0, tiled=True),
        lax.all_gather(w_down, "dp", axis=1, tiled=True),
    )
    normed_one, kept_one, inverse_one = norm_forward(mix_inputs(attn_pre, streams))
    query_raw = jnp.dot(normed_one, query_w, preferred_element_type=jnp.float32).reshape(
        shape_heads
    )
    key_raw = jnp.dot(normed_one, key_w, preferred_element_type=jnp.float32).reshape(shape_heads)
    values = (
        jnp.dot(normed_one, value_w, preferred_element_type=jnp.float32)
        .astype(jnp.bfloat16)
        .reshape(shape_heads)
    )
    queries = rotate(query_raw, cosine_table, sine_table).astype(jnp.bfloat16)
    keys_roped = rotate(key_raw, cosine_table, sine_table).astype(jnp.bfloat16)

    def forward_sequence(inputs):
        return attend_forward(
            inputs[0], inputs[1], inputs[2], inputs[3], inputs[4], inputs[5], score_scale
        )

    attended, log_sums, seq_tops = lax.map(
        forward_sequence, (queries, keys_roped, values, doc_ids, span_starts, span_lengths)
    )
    head_top = lax.pmax(jnp.max(seq_tops, axis=0), "dp")
    attended_low = attended.reshape(tokens, column_count).astype(jnp.bfloat16)
    branch_one = branch_rows(jnp.dot(attended_low, out_w, preferred_element_type=jnp.float32))
    after_attn = mix_streams(attn_mix, streams) + attn_post[:, None, None] * branch_one[None, :, :]
    normed_two, kept_two, inverse_two = norm_forward(mix_inputs(ffn_pre, after_attn))
    gate_proj = jnp.dot(normed_two, gate_w, preferred_element_type=jnp.float32)
    up_proj = jnp.dot(normed_two, up_w, preferred_element_type=jnp.float32)
    sigmoid_gate = jax.nn.sigmoid(gate_proj)
    hidden = (gate_proj * sigmoid_gate * up_proj).astype(jnp.bfloat16)
    branch_two = branch_rows(jnp.dot(hidden, down_w, preferred_element_type=jnp.float32))
    out_streams = (
        mix_streams(ffn_mix, after_attn) + ffn_post[:, None, None] * branch_two[None, :, :]
    )
    ffn_post_grad = jnp.sum(cotangent * branch_two[None, :, :], axis=(1, 2))
    ffn_mix_grad = jnp.sum(cotangent[:, None, :, :] * after_attn[None, :, :, :], axis=(2, 3))
    two_grad = features(jnp.sum(ffn_post[:, None, None] * cotangent, axis=0).astype(jnp.bfloat16))
    hidden_grad = jnp.dot(two_grad, down_w.T, preferred_element_type=jnp.float32)
    down_wgrad = jnp.einsum("tf,td->fd", hidden, two_grad, preferred_element_type=jnp.float32)
    gate_grad = (
        hidden_grad * up_proj * sigmoid_gate * (1.0 + gate_proj * (1.0 - sigmoid_gate))
    ).astype(jnp.bfloat16)
    up_grad = (hidden_grad * gate_proj * sigmoid_gate).astype(jnp.bfloat16)
    gate_wgrad = jnp.einsum("td,tf->df", normed_two, gate_grad, preferred_element_type=jnp.float32)
    up_wgrad = jnp.einsum("td,tf->df", normed_two, up_grad, preferred_element_type=jnp.float32)
    gate_shard, up_shard, down_shard = (
        lax.psum_scatter(gate_wgrad, "dp", scatter_dimension=0, tiled=True),
        lax.psum_scatter(up_wgrad, "dp", scatter_dimension=0, tiled=True),
        lax.psum_scatter(down_wgrad, "dp", scatter_dimension=1, tiled=True),
    )
    normed_two_grad = jnp.dot(gate_grad, gate_w.T, preferred_element_type=jnp.float32) + jnp.dot(
        up_grad, up_w.T, preferred_element_type=jnp.float32
    )
    h_two_grad = norm_backward(normed_two_grad, kept_two, inverse_two)
    ffn_pre_grad = jnp.sum(h_two_grad[None, :, :] * after_attn, axis=(1, 2))
    after_grad = mix_back(ffn_mix, cotangent) + ffn_pre[:, None, None] * h_two_grad[None, :, :]
    attn_post_grad = jnp.sum(after_grad * branch_one[None, :, :], axis=(1, 2))
    attn_mix_grad = jnp.sum(after_grad[:, None, :, :] * streams[None, :, :, :], axis=(2, 3))
    one_grad = features(jnp.sum(attn_post[:, None, None] * after_grad, axis=0).astype(jnp.bfloat16))
    attended_grad = jnp.dot(one_grad, out_w.T, preferred_element_type=jnp.float32).astype(
        jnp.bfloat16
    )
    out_wgrad = jnp.einsum("tc,td->cd", attended_low, one_grad, preferred_element_type=jnp.float32)

    def backward_sequence(inputs):
        return attend_backward(
            inputs[0],
            inputs[1],
            inputs[2],
            inputs[3],
            inputs[4],
            inputs[5],
            inputs[6],
            inputs[7],
            score_scale,
        )

    query_grad, key_grad, value_grad = lax.map(
        backward_sequence,
        (
            queries,
            keys_roped,
            values,
            attended_grad.reshape(shape_heads),
            log_sums,
            doc_ids,
            span_starts,
            span_lengths,
        ),
    )
    query_low = (
        rotate_back(query_grad, cosine_table, sine_table)
        .reshape(tokens, column_count)
        .astype(jnp.bfloat16)
    )
    key_low = (
        rotate_back(key_grad, cosine_table, sine_table)
        .reshape(tokens, column_count)
        .astype(jnp.bfloat16)
    )
    value_low = value_grad.reshape(tokens, column_count).astype(jnp.bfloat16)
    query_wgrad = jnp.einsum("td,tc->dc", normed_one, query_low, preferred_element_type=jnp.float32)
    key_wgrad = jnp.einsum("td,tc->dc", normed_one, key_low, preferred_element_type=jnp.float32)
    value_wgrad = jnp.einsum("td,tc->dc", normed_one, value_low, preferred_element_type=jnp.float32)
    normed_one_grad = (
        jnp.dot(query_low, query_w.T, preferred_element_type=jnp.float32)
        + jnp.dot(key_low, key_w.T, preferred_element_type=jnp.float32)
        + jnp.dot(value_low, value_w.T, preferred_element_type=jnp.float32)
    )
    h_one_grad = norm_backward(normed_one_grad, kept_one, inverse_one)
    attn_pre_grad = jnp.sum(h_one_grad[None, :, :] * streams, axis=(1, 2))
    streams_grad = mix_back(attn_mix, after_grad) + attn_pre[:, None, None] * h_one_grad[None, :, :]
    hyper_grad = lax.psum(
        jnp.stack(
            [
                hyper_rows(attn_pre_grad, attn_post_grad, attn_mix_grad),
                hyper_rows(ffn_pre_grad, ffn_post_grad, ffn_mix_grad),
            ]
        ),
        ("dp", "wide"),
    )
    query_shard, key_shard, value_shard, out_shard = (
        lax.psum_scatter(query_wgrad, "dp", scatter_dimension=0, tiled=True),
        lax.psum_scatter(key_wgrad, "dp", scatter_dimension=0, tiled=True),
        lax.psum_scatter(value_wgrad, "dp", scatter_dimension=0, tiled=True),
        lax.psum_scatter(out_wgrad, "dp", scatter_dimension=1, tiled=True),
    )
    clip_scale = jnp.sqrt(CLIP_TAU / jnp.maximum(head_top, CLIP_TAU))
    columns = jnp.repeat(clip_scale, head_size)[None, :]
    return (
        out_streams,
        streams_grad,
        query_shard,
        key_shard,
        value_shard,
        out_shard,
        gate_shard,
        up_shard,
        down_shard,
        hyper_grad,
        clip_scale,
        w_query.astype(jnp.float32) * columns,
        w_key.astype(jnp.float32) * columns,
    )


def solution(mesh):
    return jax.shard_map(
        per_device,
        mesh=mesh,
        in_specs=(
            P(None, "dp", "wide"),
            P(None, "dp", "wide"),
            P("dp", "wide"),
            P("dp", "wide"),
            P("dp", "wide"),
            P("wide", "dp"),
            P("dp", "wide"),
            P("dp", "wide"),
            P("wide", "dp"),
            P(),
            P("dp", None),
            P("dp", None),
            P("dp", None),
        ),
        out_specs=(
            P(None, "dp", "wide"),
            P(None, "dp", "wide"),
            P("dp", "wide"),
            P("dp", "wide"),
            P("dp", "wide"),
            P("wide", "dp"),
            P("dp", "wide"),
            P("dp", "wide"),
            P("wide", "dp"),
            P(),
            P("wide"),
            P("dp", "wide"),
            P("dp", "wide"),
        ),
        check_vma=False,
    )
```

profile of v0, /device:TPU:0, one launch (start us, length us, event | category | flops | bytes accessed | tf_op | source)
XLA Modules:
  0.0 1579.7 jit_solution(8456090871075567823)
XLA Ops:
  11.9 23.4 %all-reduce.3 = (f32[1024]{0:T(1024)S(1)}, f32[1024]{0:T(1024)S(1)}) all-reduce(f32[1024]{0:T(1024)S(1)} %multiply_reduce_fusion.20, f32[1024]{0:T(1024)S(1)} %get-tuple-element.312), channel_id=1, replica_groups=mesh['dp'=4,'wide'=8] {'wide'}, use_global_device_ids=true, to_apply=%region_5.6 | all-reduce | flops 2048 | bytes 16384 | tf_op jit(solution)/shard_map/psum | solution.py:151
  42.8 66.4 %all-gather.12.cloned.1.call-done = bf16[1024,2048]{1,0:T(8,128)(2,1)} async-done(((bf16[1024,256]{1,0:T(8,128)(2,1)}), bf16[1024,2048]{1,0:T(8,128)(2,1)}) %all-gather.12.cloned.1.call-update) | async-done | bytes 4194320 | tf_op jit(solution)/shard_map/all_gather | solution.py:155
  147.9 14.2 while.53
  175.5 141.2 %reduce-scatter.12.cloned.1.call-done = f32[1024,256]{1,0:T(8,128)} async-done(((f32[1024,2048]{1,0:T(8,128)}), f32[1024,256]{1,0:T(8,128)}) %reduce-scatter.12.cloned.1.call-update) | async-done | bytes 1048592 | tf_op jit(solution)/shard_map/reduce_scatter | solution.py:159
  322.2 19.7 %all-reduce.2 = (f32[1024]{0:T(1024)S(1)}, f32[1024]{0:T(1024)S(1)}) all-reduce(f32[1024]{0:T(1024)S(1)} %multiply_reduce_fusion.19, f32[1024]{0:T(1024)S(1)} %get-tuple-element.310), channel_id=1, replica_groups=mesh['dp'=4,'wide'=8] {'wide'}, use_global_device_ids=true, to_apply=%region_18.19 | all-reduce | flops 2048 | bytes 16384 | tf_op jit(solution)/shard_map/psum | solution.py:151
  351.8 77.3 %all-gather.22.cloned.1.call-done = bf16[1024,2048]{1,0:T(8,128)(2,1)} async-done(((bf16[1024,256]{1,0:T(8,128)(2,1)}), bf16[1024,2048]{1,0:T(8,128)(2,1)}) %all-gather.22.cloned.1.call-update) | async-done | bytes 4194320 | tf_op jit(solution)/shard_map/all_gather | solution.py:155
  439.1 24.3 %all-gather.26.cloned.1.call-done = bf16[2048,1024]{1,0:T(8,128)(2,1)} async-done(((bf16[512,1024]{1,0:T(8,128)(2,1)}), bf16[2048,1024]{1,0:T(8,128)(2,1)}) %all-gather.26.cloned.1.call-update) | async-done | bytes 4194320 | tf_op jit(solution)/shard_map/all_gather | solution.py:215
  475.4 23.8 %all-gather.28.cloned.1.call-done = bf16[1024,2048]{1,0:T(8,128)(2,1)} async-done(((bf16[1024,512]{1,0:T(8,128)(2,1)}), bf16[1024,2048]{1,0:T(8,128)(2,1)}) %all-gather.28.cloned.1.call-update) | async-done | bytes 4194320 | tf_op jit(solution)/shard_map/all_gather | solution.py:216
  520.7 137.2 %reduce-scatter.14.cloned.1.call-done = f32[1024,256]{1,0:T(8,128)} async-done(((f32[1024,2048]{1,0:T(8,128)}), f32[1024,256]{1,0:T(8,128)}) %reduce-scatter.14.cloned.1.call-update) | async-done | bytes 1048592 | tf_op jit(solution)/shard_map/reduce_scatter | solution.py:159
  666.3 73.4 %all-gather.30.cloned.1.call-done = bf16[1024,2048]{1,0:T(8,128)(2,1)} async-done(((bf16[1024,256]{1,0:T(8,128)(2,1)}), bf16[1024,2048]{1,0:T(8,128)(2,1)}) %all-gather.30.cloned.1.call-update) | async-done | bytes 4194320 | tf_op jit(solution)/shard_map/all_gather | solution.py:155
  739.7 12.9 multiply_convert_fusion.1
  766.6 146.1 %reduce-scatter.16.cloned.1.call-done = f32[1024,256]{1,0:T(8,128)} async-done(((f32[1024,2048]{1,0:T(8,128)}), f32[1024,256]{1,0:T(8,128)}) %reduce-scatter.16.cloned.1.call-update) | async-done | bytes 1048592 | tf_op jit(solution)/shard_map/reduce_scatter | solution.py:175
  914.6 19.9 %all-reduce.1 = (f32[1024]{0:T(1024)S(1)}, f32[1024]{0:T(1024)S(1)}) all-reduce(f32[1024]{0:T(1024)S(1)} %get-tuple-element.326, f32[1024]{0:T(1024)S(1)} %get-tuple-element.325), channel_id=1, replica_groups=mesh['dp'=4,'wide'=8] {'wide'}, use_global_device_ids=true, to_apply=%region_26.27 | all-reduce | flops 2048 | bytes 16384 | tf_op jit(solution)/shard_map/psum | solution.py:151
  948.7 68.3 %all-gather.32.cloned.1.call-done = bf16[1024,2048]{1,0:T(8,128)(2,1)} async-done(((bf16[1024,256]{1,0:T(8,128)(2,1)}), bf16[1024,2048]{1,0:T(8,128)(2,1)}) %all-gather.32.cloned.1.call-update) | async-done | bytes 4194320 | tf_op jit(solution)/shard_map/all_gather | solution.py:155
  1020.7 30.5 %while.54 = (s32[]{:T(128)}, f32[1024,2,128]{0,2,1:T(8,128)S(1)}, f32[1024,2,128]{0,2,1:T(8,128)}, f32[2,512,2,128]{3,1,2,0:T(8,128)}, s32[2]{0:T(128)S(1)}, /*i...) while((s32[]{:T(128)}, f32[1024,2,128]{0,2,1:T(8,128)S(1)}, ...), condition=%wide.region_31.32_spmd.clone.clone, body=%wide.region_29.31_spmd.clone.sunk.clone | while | flops 1357250560 | bytes 90224648 | solution.py:144
  1135.9 76.0 %reduce-scatter.18.cloned.1.call-done = f32[1024,256]{1,0:T(8,128)} async-done(((f32[1024,2048]{1,0:T(8,128)}), f32[1024,256]{1,0:T(8,128)}) %reduce-scatter.18.cloned.1.call-update) | async-done | bytes 1048592 | tf_op jit(solution)/shard_map/reduce_scatter | solution.py:175
  1213.8 19.7 %all-reduce = (f32[1024]{0:T(1024)S(1)}, f32[1024]{0:T(1024)S(1)}) all-reduce(f32[1024]{0:T(1024)S(1)} %get-tuple-element.324, f32[1024]{0:T(1024)S(1)} %get-tuple-element.323), channel_id=1, replica_groups=mesh['dp'=4,'wide'=8] {'wide'}, use_global_device_ids=true, to_apply=%region_36.37 | all-reduce | flops 2048 | bytes 16384 | tf_op jit(solution)/shard_map/psum | solution.py:151
  1242.9 38.0 %psum.71 = f32[2,4,6]{2,1,0:T(4,128)} all-reduce(f32[2,4,6]{2,1,0:T(4,128)S(1)} %pad_maximum_fusion.3), channel_id=1, replica_groups=mesh['dp'=4,'wide'=8] {'dp','wide'}, use_global_device_ids=true, to_apply=%region_50.51 | all-reduce | flops 48 | bytes 384 | tf_op jit(solution)/shard_map/psum | solution.py:330
  1286.7 74.4 %reduce-scatter.28.cloned.1.call-done = f32[512,1024]{1,0:T(8,128)} async-done(((f32[2048,1024]{1,0:T(8,128)}), f32[512,1024]{1,0:T(8,128)}) %reduce-scatter.28.cloned.1.call-update) | async-done | bytes 2097168 | tf_op jit(solution)/shard_map/reduce_scatter | solution.py:264
  1361.1 74.4 %reduce-scatter.30.cloned.1.call-done = f32[512,1024]{1,0:T(8,128)} async-done(((f32[2048,1024]{1,0:T(8,128)}), f32[512,1024]{1,0:T(8,128)}) %reduce-scatter.30.cloned.1.call-update) | async-done | bytes 2097168 | tf_op jit(solution)/shard_map/reduce_scatter | solution.py:265
  1435.6 34.3 %reduce-scatter.22.cloned.1.call-done = f32[512,256]{1,0:T(8,128)} async-done(((f32[2048,256]{1,0:T(8,128)}), f32[512,256]{1,0:T(8,128)}) %reduce-scatter.22.cloned.1.call-update) | async-done | bytes 524304 | tf_op jit(solution)/shard_map/reduce_scatter | solution.py:341
  1469.9 34.2 %reduce-scatter.20.cloned.1.call-done = f32[512,256]{1,0:T(8,128)} async-done(((f32[2048,256]{1,0:T(8,128)}), f32[512,256]{1,0:T(8,128)}) %reduce-scatter.20.cloned.1.call-update) | async-done | bytes 524304 | tf_op jit(solution)/shard_map/reduce_scatter | solution.py:340
  1504.0 34.3 %reduce-scatter.26.cloned.1.call-done = f32[256,512]{1,0:T(8,128)} async-done(((f32[256,2048]{1,0:T(8,128)}), f32[256,512]{1,0:T(8,128)}) %reduce-scatter.26.cloned.1.call-update) | async-done | bytes 524304 | tf_op jit(solution)/shard_map/reduce_scatter | solution.py:343
  1538.4 34.3 %reduce-scatter.24.cloned.1.call-done = f32[512,256]{1,0:T(8,128)} async-done(((f32[2048,256]{1,0:T(8,128)}), f32[512,256]{1,0:T(8,128)}) %reduce-scatter.24.cloned.1.call-update) | async-done | bytes 524304 | tf_op jit(solution)/shard_map/reduce_scatter | solution.py:342
  (302 shorter events, 307.1 us)
Async XLA Ops:
  7.2 35.6 %all-gather.16.cloned.1.call-start = ((), (), s32[]{:S(2)}) async-start(), calls=%async_computation.13 | async-start | bytes 1310720 | tf_op jit(solution)/shard_map/all_gather | solution.py:209
  7.9 101.3 %all-gather.12.cloned.1.call-start = ((), (), s32[]{:S(2)}) async-start(), calls=%async_computation.11 | async-start | bytes 4718592 | tf_op jit(solution)/shard_map/all_gather | solution.py:155
  37.1 88.5 %all-gather.14.cloned.1.call-start = ((), (), s32[]{:S(2)}) async-start(), calls=%async_computation.12 | async-start | bytes 1310720 | tf_op jit(solution)/shard_map/all_gather | solution.py:208
  37.9 105.9 %all-gather.18.cloned.1.call-start = ((), (), s32[]{:S(2)}) async-start(), calls=%async_computation.14 | async-start | bytes 1310720 | tf_op jit(solution)/shard_map/all_gather | solution.py:210
  38.5 124.3 %all-gather.20.cloned.1.call-start = ((), (), s32[]{:S(2)}) async-start(), calls=%async_computation.15 | async-start | bytes 1310720 | tf_op jit(solution)/shard_map/all_gather | solution.py:211
  39.0 277.6 %reduce-scatter.12.cloned.1.call-start = ((), (), s32[]{:S(2)}) async-start(), calls=%async_computation.16 | async-start | bytes 9437184 | tf_op jit(solution)/shard_map/reduce_scatter | solution.py:159
  42.5 902.6 %copy-start.12 = (f32[1024,128]{0,1:T(8,128)}, f32[1024,128]{0,1:T(8,128)S(1)}, u32[]{:S(2)}) copy-start(f32[1024,128]{0,1:T(8,128)S(1)} %copy.61) | copy-start | bytes 1572868
  168.6 183.2 %all-gather.24.cloned.1.call-start = ((), (), s32[]{:S(2)}) async-start(), calls=%async_computation.18 | async-start | bytes 5242880 | tf_op jit(solution)/shard_map/all_gather | solution.py:214
  169.4 259.7 %all-gather.22.cloned.1.call-start = ((), (), s32[]{:S(2)}) async-start(), calls=%async_computation.17 | async-start | bytes 4718592 | tf_op jit(solution)/shard_map/all_gather | solution.py:155
  343.1 120.2 %all-gather.26.cloned.1.call-start = ((), (), s32[]{:S(2)}) async-start(), calls=%async_computation.19 | async-start | bytes 5242880 | tf_op jit(solution)/shard_map/all_gather | solution.py:215
  343.8 155.4 %all-gather.28.cloned.1.call-start = ((), (), s32[]{:S(2)}) async-start(), calls=%async_computation.20 | async-start | bytes 5242880 | tf_op jit(solution)/shard_map/all_gather | solution.py:216
  344.4 313.4 %reduce-scatter.14.cloned.1.call-start = ((), (), s32[]{:S(2)}) async-start(), calls=%async_computation.21 | async-start | bytes 9437184 | tf_op jit(solution)/shard_map/reduce_scatter | solution.py:159
  509.8 229.9 %all-gather.30.cloned.1.call-start = ((), (), s32[]{:S(2)}) async-start(), calls=%async_computation.22 | async-start | bytes 4718592 | tf_op jit(solution)/shard_map/all_gather | solution.py:155
  665.9 246.9 %reduce-scatter.16.cloned.1.call-start = ((), (), s32[]{:S(2)}) async-start(), calls=%async_computation.23 | async-start | bytes 9437184 | tf_op jit(solution)/shard_map/reduce_scatter | solution.py:175
  766.6 250.4 %all-gather.32.cloned.1.call-start = ((), (), s32[]{:S(2)}) async-start(), calls=%async_computation.24 | async-start | bytes 4718592 | tf_op jit(solution)/shard_map/all_gather | solution.py:155
  944.9 267.0 %reduce-scatter.18.cloned.1.call-start = ((), (), s32[]{:S(2)}) async-start(), calls=%async_computation.25 | async-start | bytes 9437184 | tf_op jit(solution)/shard_map/reduce_scatter | solution.py:175
  1065.7 221.0 %reduce-scatter.32.cloned.1.call-start = ((), (), s32[]{:S(2)}) async-start(), calls=%async_computation.32 | async-start | bytes 10485760 | tf_op jit(solution)/shard_map/reduce_scatter | solution.py:266
  1076.6 284.5 %reduce-scatter.28.cloned.1.call-start = ((), (), s32[]{:S(2)}) async-start(), calls=%async_computation.30 | async-start | bytes 10485760 | tf_op jit(solution)/shard_map/reduce_scatter | solution.py:264
  1087.4 348.2 %reduce-scatter.30.cloned.1.call-start = ((), (), s32[]{:S(2)}) async-start(), calls=%async_computation.31 | async-start | bytes 10485760 | tf_op jit(solution)/shard_map/reduce_scatter | solution.py:265
  1098.6 371.3 %reduce-scatter.22.cloned.1.call-start = ((), (), s32[]{:S(2)}) async-start(), calls=%async_computation.27 | async-start | bytes 2621440 | tf_op jit(solution)/shard_map/reduce_scatter | solution.py:341
  1103.5 400.5 %reduce-scatter.20.cloned.1.call-start = ((), (), s32[]{:S(2)}) async-start(), calls=%async_computation.26 | async-start | bytes 2621440 | tf_op jit(solution)/shard_map/reduce_scatter | solution.py:340
  1108.6 429.7 %reduce-scatter.26.cloned.1.call-start = ((), (), s32[]{:S(2)}) async-start(), calls=%async_computation.29 | async-start | bytes 2621440 | tf_op jit(solution)/shard_map/reduce_scatter | solution.py:343
  1113.9 458.8 %reduce-scatter.24.cloned.1.call-start = ((), (), s32[]{:S(2)}) async-start(), calls=%async_computation.28 | async-start | bytes 2621440 | tf_op jit(solution)/shard_map/reduce_scatter | solution.py:342
  1135.9 99.5 %copy-start.39 = (f32[4]{0:T(128)S(1)}, f32[4]{0:T(128)}, u32[]{:S(2)}) copy-start(f32[4]{0:T(128)} %copy-done.38) | copy-start | bytes 52
  (57 other events, 722.8 us)
Sparse Core Ops, SparseCore 0:
  9.5 19.4 all-gather.15
  37.3 71.8 all-gather.11
  110.8 14.8 all-gather.13
  127.1 16.6 all-gather.17
  145.2 16.6 all-gather.19
  168.7 147.8 reduce-scatter.11
  318.2 33.5 all-gather.23
  354.4 74.6 all-gather.21
  430.7 32.6 all-gather.25
  464.7 34.4 all-gather.27
  509.9 147.8 reduce-scatter.13
  666.0 73.7 all-gather.29
  766.7 146.0 reduce-scatter.15
  945.1 71.8 all-gather.31
  1065.9 146.0 reduce-scatter.17
  1214.9 71.7 reduce-scatter.31
  1289.7 71.3 reduce-scatter.27
  1364.1 71.3 reduce-scatter.29
  1438.7 31.1 reduce-scatter.21
  1472.8 31.1 reduce-scatter.19
  1507.2 31.1 reduce-scatter.25
  1541.5 31.1 reduce-scatter.23
where the time goes:
time: 1590 us; the launch traced here: 1580 us
  waiting for transfers between devices  1160 us (73%)
  matrix products  165 us (10%)
  blocking collectives  127 us (8%)
  other arithmetic  86.2 us (5%)
  local copies, waits for them, and re-layouts  21 us (1%)
    all_gather x4, waiting for transfers between devices, features(): return lax.all_gather(piece, 'wide', axis=1, tiled=True)  285 us
    reduce_scatter x2, waiting for transfers between devices, branch_rows(): lax.psum_scatter(partial_value, 'wide', scatter_dimension=1, tiled=True)  278 us
    reduce_scatter x2, waiting for transfers between devices, norm_backward(): lax.psum_scatter(partial_value, 'wide', scatter_dimension=1, tiled=True)  222 us
    psum x4, blocking collectives, row_sums(): lax.psum((jnp.sum(first_term, axis=1), jnp.sum(second_term, axis=1)), 'wi...  82.8 us
    reduce_scatter x1, waiting for transfers between devices, per_device(): lax.psum_scatter(up_wgrad, 'dp', scatter_dimension=0, tiled=True)  74.4 us
    reduce_scatter x1, waiting for transfers between devices, per_device(): lax.psum_scatter(gate_wgrad, 'dp', scatter_dimension=0, tiled=True)  74.4 us
    psum x1, blocking collectives, per_device(): lax.psum(jnp.stack([hyper_rows(attn_pre_grad, attn_post_grad, attn_mix_gr...  38 us
    reduce_scatter x1, waiting for transfers between devices, per_device(): lax.psum_scatter(out_wgrad, 'dp', scatter_dimension=1, tiled=True)  34.3 us
  transfers between devices with their start and end apart: 22, of which 20 were waited for; matrix products, arithmetic and copies ran while one was open for 10% of the time, Pallas kernels for 0%

commit v1 on v0

--- a/solution.py
+++ b/solution.py
@@ -1,3 +1,4 @@
+import functools
 import math
 import jax
 import jax.numpy as jnp
@@ -9,6 +10,24 @@
 CLIP_TAU = 6
 EPSILON = 1e-05
 MASKED = -1e30
+
+
+def apply_blocks(local, axis_key):
+    tall = lax.psum(1, axis_name=axis_key)
+    all_values = lax.axis_index(axis_key)
+    b_next, block_next = (tall, all_values)
+    r1, found_now = (local, 1)
+    while found_now < b_next:
+        state_now = tuple(((d, d ^ found_now) for d in range(b_next)))
+        w1 = lax.ppermute(r1, axis_key, state_now)
+        o_now = jnp.concatenate([r1, w1], axis=1)
+        ready = jnp.concatenate([w1, r1], axis=1)
+        r1 = jnp.where(block_next & found_now == 0, o_now, ready)
+        found_now = 2 * found_now
+    return r1
+
+
+points_recover = functools.partial(apply_blocks, axis_key="wide")
 
 
 def rope_tables(length, head_size):
@@ -152,7 +171,7 @@
 
 
 def features(piece):
-    return lax.all_gather(piece, "wide", axis=1, tiled=True)
+    return points_recover(piece)
 
 
 def branch_rows(partial_value):

time: 1590 us -> 1700 us (1.069)
  waiting for transfers between devices: 1160 us -> 1250 us
    ppermute x0 -> x12, waiting for transfers between devices: none -> 470 us  [apply_blocks(): w1 = lax.ppermute(r1, axis_key, state_now)]
    all_gather x4 -> x0, waiting for transfers between devices: 285 us -> none  [features(): return lax.all_gather(piece, 'wide', axis=1, tiled=True)]
    all_gather x1, waiting for transfers between devices: 24.3 us -> 0.01 us  [per_device(): lax.all_gather(w_up, 'dp', axis=0, tiled=True)]
    all_gather x1, waiting for transfers between devices: 23.8 us -> 0.01 us  [per_device(): lax.all_gather(w_down, 'dp', axis=1, tiled=True)]
  transfers between devices with their start and end apart: 22 -> 30, of which waited for: 20 -> 23; matrix products, arithmetic and copies ran while one was open for 10% -> 10% of each run, Pallas kernels for 0% -> 0%
where the time goes in v1:
time: 1700 us
  waiting for transfers between devices  1250 us (74%)
  matrix products  169 us (10%)
  blocking collectives  128 us (8%)
  other arithmetic  98.7 us (6%)
  local copies, waits for them, and re-layouts  22.8 us (1%)
    ppermute x12, waiting for transfers between devices, apply_blocks(): w1 = lax.ppermute(r1, axis_key, state_now)  470 us
    reduce_scatter x2, waiting for transfers between devices, branch_rows(): lax.psum_scatter(partial_value, 'wide', scatter_dimension=1, tiled=True)  271 us
    reduce_scatter x2, waiting for transfers between devices, norm_backward(): lax.psum_scatter(partial_value, 'wide', scatter_dimension=1, tiled=True)  217 us
    psum x4, blocking collectives, row_sums(): lax.psum((jnp.sum(first_term, axis=1), jnp.sum(second_term, axis=1)), 'wi...  82.8 us
    reduce_scatter x1, waiting for transfers between devices, per_device(): lax.psum_scatter(up_wgrad, 'dp', scatter_dimension=0, tiled=True)  74.6 us
    reduce_scatter x1, waiting for transfers between devices, per_device(): lax.psum_scatter(gate_wgrad, 'dp', scatter_dimension=0, tiled=True)  74.4 us
    psum x1, blocking collectives, per_device(): lax.psum(jnp.stack([hyper_rows(attn_pre_grad, attn_post_grad, attn_mix_gr...  38 us
    reduce_scatter x1, waiting for transfers between devices, per_device(): lax.psum_scatter(key_wgrad, 'dp', scatter_dimension=0, tiled=True)  34.2 us
  transfers between devices with their start and end apart: 30, of which 23 were waited for; matrix products, arithmetic and copies ran while one was open for 10% of the time, Pallas kernels for 0%

profile of v1, /device:TPU:0, one launch (start us, length us, event | category | flops | bytes accessed | tf_op | source)
XLA Modules:
  0.0 1696.5 jit_solution(12485429996054742657)
XLA Ops:
  12.7 23.5 %all-reduce.3 = (f32[1024]{0:T(1024)S(1)}, f32[1024]{0:T(1024)S(1)}) all-reduce(f32[1024]{0:T(1024)S(1)} %multiply_reduce_fusion.20, f32[1024]{0:T(1024)S(1)} %get-tuple-element.312), channel_id=1, replica_groups=mesh['dp'=4,'wide'=8] {'wide'}, use_global_device_ids=true, to_apply=%region_5.6 | all-reduce | flops 2048 | bytes 16384 | tf_op jit(solution)/shard_map/psum | solution.py:170
  47.8 19.6 %collective-permute-done.1 = bf16[1024,512]{1,0:T(8,128)(2,1)} collective-permute-done((bf16[1024,512]{1,0:T(8,128)(2,1)S(1)}, bf16[1024,512]{1,0:T(8,128)(2,1)}, u32[]{:S(2)}, u32[]{:S(2)}) %collective-permute-start.1) | collective-permute-done | bytes 1048608 | tf_op jit(solution)/shard_map/ppermute | solution.py:22
  76.3 82.1 %collective-permute-done.2 = bf16[1024,1024]{1,0:T(8,128)(2,1)} collective-permute-done((bf16[1024,1024]{1,0:T(8,128)(2,1)S(1)}, bf16[1024,1024]{1,0:T(8,128)(2,1)}, u32[]{:S(2)}, u32[]{:S(2)}) %collective-permute-start.2) | collective-permute-done | bytes 2097184 | tf_op jit(solution)/shard_map/ppermute | solution.py:22
  205.9 137.6 %reduce-scatter.12.cloned.1.call-done = f32[1024,256]{1,0:T(8,128)} async-done(((f32[1024,2048]{1,0:T(8,128)}), f32[1024,256]{1,0:T(8,128)}) %reduce-scatter.12.cloned.1.call-update) | async-done | bytes 1048592 | tf_op jit(solution)/shard_map/reduce_scatter | solution.py:178
  349.0 19.8 %all-reduce.2 = (f32[1024]{0:T(1024)S(1)}, f32[1024]{0:T(1024)S(1)}) all-reduce(f32[1024]{0:T(1024)S(1)} %multiply_reduce_fusion.19, f32[1024]{0:T(1024)S(1)} %get-tuple-element.310), channel_id=1, replica_groups=mesh['dp'=4,'wide'=8] {'wide'}, use_global_device_ids=true, to_apply=%region_18.19 | all-reduce | flops 2048 | bytes 16384 | tf_op jit(solution)/shard_map/psum | solution.py:170
  381.0 20.5 %collective-permute-done.4 = bf16[1024,512]{1,0:T(8,128)(2,1)S(1)} collective-permute-done((bf16[1024,512]{1,0:T(8,128)(2,1)S(1)}, bf16[1024,512]{1,0:T(8,128)(2,1)S(1)}, u32[]{:S(2)}, u32[]{:S(2)}) %collective-permute-start.4) | collective-permute-done | bytes 1048608 | tf_op jit(solution)/shard_map/ppermute | solution.py:22
  403.5 88.4 %collective-permute-done.5 = bf16[1024,1024]{1,0:T(8,128)(2,1)} collective-permute-done((bf16[1024,1024]{1,0:T(8,128)(2,1)}, bf16[1024,1024]{1,0:T(8,128)(2,1)}, u32[]{:S(2)}, u32[]{:S(2)}) %collective-permute-start.5) | collective-permute-done | bytes 2097184 | tf_op jit(solution)/shard_map/ppermute | solution.py:22
  536.1 133.6 %reduce-scatter.14.cloned.1.call-done = f32[1024,256]{1,0:T(8,128)} async-done(((f32[1024,2048]{1,0:T(8,128)}), f32[1024,256]{1,0:T(8,128)}) %reduce-scatter.14.cloned.1.call-update) | async-done | bytes 1048592 | tf_op jit(solution)/shard_map/reduce_scatter | solution.py:178
  691.4 23.4 %collective-permute-done.7 = bf16[1024,512]{1,0:T(8,128)(2,1)S(1)} collective-permute-done((bf16[1024,512]{1,0:T(8,128)(2,1)S(1)}, bf16[1024,512]{1,0:T(8,128)(2,1)S(1)}, u32[]{:S(2)}, u32[]{:S(2)}) %collective-permute-start.7) | collective-permute-done | bytes 1048608 | tf_op jit(solution)/shard_map/ppermute | solution.py:22
  717.4 89.2 %collective-permute-done.8 = bf16[1024,1024]{1,0:T(8,128)(2,1)S(1)} collective-permute-done((bf16[1024,1024]{1,0:T(8,128)(2,1)S(1)}, bf16[1024,1024]{1,0:T(8,128)(2,1)S(1)}, u32[]{:S(2)}, u32[]{:S(2)}) %collective-permute-start.8) | collective-permute-done | bytes 2097184 | tf_op jit(solution)/shard_map/ppermute | solution.py:22
  831.6 148.7 %reduce-scatter.16.cloned.1.call-done = f32[1024,256]{1,0:T(8,128)} async-done(((f32[1024,2048]{1,0:T(8,128)}), f32[1024,256]{1,0:T(8,128)}) %reduce-scatter.16.cloned.1.call-update) | async-done | bytes 1048592 | tf_op jit(solution)/shard_map/reduce_scatter | solution.py:194
  982.1 19.7 %all-reduce.1 = (f32[1024]{0:T(1024)S(1)}, f32[1024]{0:T(1024)S(1)}) all-reduce(f32[1024]{0:T(1024)S(1)} %get-tuple-element.326, f32[1024]{0:T(1024)S(1)} %get-tuple-element.325), channel_id=1, replica_groups=mesh['dp'=4,'wide'=8] {'wide'}, use_global_device_ids=true, to_apply=%region_26.27 | all-reduce | flops 2048 | bytes 16384 | tf_op jit(solution)/shard_map/psum | solution.py:170
  1021.9 20.5 %collective-permute-done.10 = bf16[1024,512]{1,0:T(8,128)(2,1)S(1)} collective-permute-done((bf16[1024,512]{1,0:T(8,128)(2,1)S(1)}, bf16[1024,512]{1,0:T(8,128)(2,1)S(1)}, u32[]{:S(2)}, u32[]{:S(2)}) %collective-permute-start.10) | collective-permute-done | bytes 1048608 | tf_op jit(solution)/shard_map/ppermute | solution.py:22
  1048.1 84.7 %collective-permute-done.11 = bf16[1024,1024]{1,0:T(8,128)(2,1)} collective-permute-done((bf16[1024,1024]{1,0:T(8,128)(2,1)}, bf16[1024,1024]{1,0:T(8,128)(2,1)}, u32[]{:S(2)}, u32[]{:S(2)}) %collective-permute-start.11) | collective-permute-done | bytes 2097184 | tf_op jit(solution)/shard_map/ppermute | solution.py:22
  1138.0 30.9 %while.54 = (s32[]{:T(128)}, f32[1024,2,128]{0,2,1:T(8,128)S(1)}, f32[1024,2,128]{0,2,1:T(8,128)}, f32[2,512,2,128]{3,1,2,0:T(8,128)}, s32[2]{0:T(128)S(1)}, /*i...) while((s32[]{:T(128)}, f32[1024,2,128]{0,2,1:T(8,128)S(1)}, ...), condition=%wide.region_31.32_spmd.clone.clone, body=%wide.region_29.31_spmd.clone.sunk.clone | while | flops 1357250560 | bytes 90224648 | solution.py:163
  1260.8 68.2 %reduce-scatter.18.cloned.1.call-done = f32[1024,256]{1,0:T(8,128)} async-done(((f32[1024,2048]{1,0:T(8,128)}), f32[1024,256]{1,0:T(8,128)}) %reduce-scatter.18.cloned.1.call-update) | async-done | bytes 1048592 | tf_op jit(solution)/shard_map/reduce_scatter | solution.py:194
  1330.9 19.7 %all-reduce = (f32[1024]{0:T(1024)S(1)}, f32[1024]{0:T(1024)S(1)}) all-reduce(f32[1024]{0:T(1024)S(1)} %get-tuple-element.324, f32[1024]{0:T(1024)S(1)} %get-tuple-element.323), channel_id=1, replica_groups=mesh['dp'=4,'wide'=8] {'wide'}, use_global_device_ids=true, to_apply=%region_36.37 | all-reduce | flops 2048 | bytes 16384 | tf_op jit(solution)/shard_map/psum | solution.py:170
  1359.9 38.0 %psum.71 = f32[2,4,6]{2,1,0:T(4,128)} all-reduce(f32[2,4,6]{2,1,0:T(4,128)S(1)} %pad_maximum_fusion.3), channel_id=1, replica_groups=mesh['dp'=4,'wide'=8] {'dp','wide'}, use_global_device_ids=true, to_apply=%region_50.51 | all-reduce | flops 48 | bytes 384 | tf_op jit(solution)/shard_map/psum | solution.py:349
  1403.8 74.6 %reduce-scatter.30.cloned.1.call-done = f32[512,1024]{1,0:T(8,128)} async-done(((f32[2048,1024]{1,0:T(8,128)}), f32[512,1024]{1,0:T(8,128)}) %reduce-scatter.30.cloned.1.call-update) | async-done | bytes 2097168 | tf_op jit(solution)/shard_map/reduce_scatter | solution.py:284
  1478.3 74.4 %reduce-scatter.28.cloned.1.call-done = f32[512,1024]{1,0:T(8,128)} async-done(((f32[2048,1024]{1,0:T(8,128)}), f32[512,1024]{1,0:T(8,128)}) %reduce-scatter.28.cloned.1.call-update) | async-done | bytes 2097168 | tf_op jit(solution)/shard_map/reduce_scatter | solution.py:283
  1552.8 34.2 %reduce-scatter.26.cloned.1.call-done = f32[256,512]{1,0:T(8,128)} async-done(((f32[256,2048]{1,0:T(8,128)}), f32[256,512]{1,0:T(8,128)}) %reduce-scatter.26.cloned.1.call-update) | async-done | bytes 524304 | tf_op jit(solution)/shard_map/reduce_scatter | solution.py:362
  1586.9 34.2 %reduce-scatter.22.cloned.1.call-done = f32[512,256]{1,0:T(8,128)} async-done(((f32[2048,256]{1,0:T(8,128)}), f32[512,256]{1,0:T(8,128)}) %reduce-scatter.22.cloned.1.call-update) | async-done | bytes 524304 | tf_op jit(solution)/shard_map/reduce_scatter | solution.py:360
  1621.1 34.2 %reduce-scatter.20.cloned.1.call-done = f32[512,256]{1,0:T(8,128)} async-done(((f32[2048,256]{1,0:T(8,128)}), f32[512,256]{1,0:T(8,128)}) %reduce-scatter.20.cloned.1.call-update) | async-done | bytes 524304 | tf_op jit(solution)/shard_map/reduce_scatter | solution.py:359
  1655.3 34.2 %reduce-scatter.24.cloned.1.call-done = f32[512,256]{1,0:T(8,128)} async-done(((f32[2048,256]{1,0:T(8,128)}), f32[512,256]{1,0:T(8,128)}) %reduce-scatter.24.cloned.1.call-update) | async-done | bytes 524304 | tf_op jit(solution)/shard_map/reduce_scatter | solution.py:361
  (331 shorter events, 368.3 us)
Async XLA Ops:
  7.2 156.6 %all-gather.10.cloned.1.call-start = ((), (), s32[]{:S(2)}) async-start(), calls=%async_computation.12 | async-start | bytes 1310720 | tf_op jit(solution)/shard_map/all_gather | solution.py:228
  7.9 160.6 %all-gather.8.cloned.1.call-start = ((), (), s32[]{:S(2)}) async-start(), calls=%async_computation.11 | async-start | bytes 1310720 | tf_op jit(solution)/shard_map/all_gather | solution.py:227
  8.7 165.2 %all-gather.12.cloned.1.call-start = ((), (), s32[]{:S(2)}) async-start(), calls=%async_computation.13 | async-start | bytes 1310720 | tf_op jit(solution)/shard_map/all_gather | solution.py:229
  46.9 145.4 %all-gather.14.cloned.1.call-start = ((), (), s32[]{:S(2)}) async-start(), calls=%async_computation.14 | async-start | bytes 1310720 | tf_op jit(solution)/shard_map/all_gather | solution.py:230
  70.4 88.0 %collective-permute-start.2 = (bf16[1024,1024]{1,0:T(8,128)(2,1)S(1)}, bf16[1024,1024]{1,0:T(8,128)(2,1)}, u32[]{:S(2)}, u32[]{:S(2)}) collective-permute-start(bf16[1024,1024]{1,0:T(8,128)(2,1)S(1)} %maximum_select_fusion.4), channel_id=1, source_target_pairs={{0,4},{1,5},{2,6},{3,7},{4,0},{5,1},{6,2},{7,3},{8,12},{9,13},{10,... | collective-permute-start | bytes 6291464 | tf_op jit(solution)/shard_map/ppermute | solution.py:22
  70.5 273.0 %reduce-scatter.12.cloned.1.call-start = ((), (), s32[]{:S(2)}) async-start(), calls=%async_computation.15 | async-start | bytes 9437184 | tf_op jit(solution)/shard_map/reduce_scatter | solution.py:178
  198.2 205.3 %all-gather.16.cloned.1.call-start = ((), (), s32[]{:S(2)}) async-start(), calls=%async_computation.16 | async-start | bytes 5242880 | tf_op jit(solution)/shard_map/all_gather | solution.py:233
  198.8 304.3 %all-gather.18.cloned.1.call-start = ((), (), s32[]{:S(2)}) async-start(), calls=%async_computation.17 | async-start | bytes 5242880 | tf_op jit(solution)/shard_map/all_gather | solution.py:234
  199.5 314.2 %all-gather.20.cloned.1.call-start = ((), (), s32[]{:S(2)}) async-start(), calls=%async_computation.18 | async-start | bytes 5242880 | tf_op jit(solution)/shard_map/all_gather | solution.py:235
  369.3 300.5 %reduce-scatter.14.cloned.1.call-start = ((), (), s32[]{:S(2)}) async-start(), calls=%async_computation.19 | async-start | bytes 9437184 | tf_op jit(solution)/shard_map/reduce_scatter | solution.py:178
  403.5 88.4 %collective-permute-start.5 = (bf16[1024,1024]{1,0:T(8,128)(2,1)}, bf16[1024,1024]{1,0:T(8,128)(2,1)}, u32[]{:S(2)}, u32[]{:S(2)}) collective-permute-start(bf16[1024,1024]{1,0:T(8,128)(2,1)} %maximum_select_fusion.5), channel_id=1, source_target_pairs={{0,4},{1,5},{2,6},{3,7},{4,0},{5,1},{6,2},{7,3},{8,12},{9,13},{10,... | collective-permute-start | bytes 6291464 | tf_op jit(solution)/shard_map/ppermute | solution.py:22
  524.3 456.0 %reduce-scatter.16.cloned.1.call-start = ((), (), s32[]{:S(2)}) async-start(), calls=%async_computation.20 | async-start | bytes 9437184 | tf_op jit(solution)/shard_map/reduce_scatter | solution.py:194
  690.9 23.8 %collective-permute-start.7 = (bf16[1024,512]{1,0:T(8,128)(2,1)S(1)}, bf16[1024,512]{1,0:T(8,128)(2,1)S(1)}, u32[]{:S(2)}, u32[]{:S(2)}) collective-permute-start(bf16[1024,512]{1,0:T(8,128)(2,1)S(1)} %maximum_select_fusion.10), channel_id=1, source_target_pairs={{0,2},{1,3},{2,0},{3,1},{4,6},{5,7},{6,4},{7,5},{8,10},{9,11},{10,... | collective-permute-start | bytes 3145736 | tf_op jit(solution)/shard_map/ppermute | solution.py:22
  715.4 91.3 %collective-permute-start.8 = (bf16[1024,1024]{1,0:T(8,128)(2,1)S(1)}, bf16[1024,1024]{1,0:T(8,128)(2,1)S(1)}, u32[]{:S(2)}, u32[]{:S(2)}) collective-permute-start(bf16[1024,1024]{1,0:T(8,128)(2,1)S(1)} %maximum_select_fusion.6), channel_id=1, source_target_pairs={{0,4},{1,5},{2,6},{3,7},{4,0},{5,1},{6,2},{7,3},{8,12},{9,13},{10,... | collective-permute-start | bytes 6291464 | tf_op jit(solution)/shard_map/ppermute | solution.py:22
  831.6 497.4 %reduce-scatter.18.cloned.1.call-start = ((), (), s32[]{:S(2)}) async-start(), calls=%async_computation.21 | async-start | bytes 9437184 | tf_op jit(solution)/shard_map/reduce_scatter | solution.py:194
  1021.8 20.6 %collective-permute-start.10 = (bf16[1024,512]{1,0:T(8,128)(2,1)S(1)}, bf16[1024,512]{1,0:T(8,128)(2,1)S(1)}, u32[]{:S(2)}, u32[]{:S(2)}) collective-permute-start(bf16[1024,512]{1,0:T(8,128)(2,1)S(1)} %maximum_select_fusion.11), channel_id=1, source_target_pairs={{0,2},{1,3},{2,0},{3,1},{4,6},{5,7},{6,4},{7,5},{8,10},{9,11},{10,... | collective-permute-start | bytes 3145736 | tf_op jit(solution)/shard_map/ppermute | solution.py:22
  1044.4 88.3 %collective-permute-start.11 = (bf16[1024,1024]{1,0:T(8,128)(2,1)}, bf16[1024,1024]{1,0:T(8,128)(2,1)}, u32[]{:S(2)}, u32[]{:S(2)}) collective-permute-start(bf16[1024,1024]{1,0:T(8,128)(2,1)} %maximum_select_fusion.7), channel_id=1, source_target_pairs={{0,4},{1,5},{2,6},{3,7},{4,0},{5,1},{6,2},{7,3},{8,12},{9,13},{10,... | collective-permute-start | bytes 6291464 | tf_op jit(solution)/shard_map/ppermute | solution.py:22
  1183.4 220.4 %reduce-scatter.32.cloned.1.call-start = ((), (), s32[]{:S(2)}) async-start(), calls=%async_computation.28 | async-start | bytes 10485760 | tf_op jit(solution)/shard_map/reduce_scatter | solution.py:285
  1195.4 283.0 %reduce-scatter.30.cloned.1.call-start = ((), (), s32[]{:S(2)}) async-start(), calls=%async_computation.27 | async-start | bytes 10485760 | tf_op jit(solution)/shard_map/reduce_scatter | solution.py:284
  1207.8 345.0 %reduce-scatter.28.cloned.1.call-start = ((), (), s32[]{:S(2)}) async-start(), calls=%async_computation.26 | async-start | bytes 10485760 | tf_op jit(solution)/shard_map/reduce_scatter | solution.py:283
  1220.1 366.9 %reduce-scatter.26.cloned.1.call-start = ((), (), s32[]{:S(2)}) async-start(), calls=%async_computation.25 | async-start | bytes 2621440 | tf_op jit(solution)/shard_map/reduce_scatter | solution.py:362
  1227.6 393.5 %reduce-scatter.22.cloned.1.call-start = ((), (), s32[]{:S(2)}) async-start(), calls=%async_computation.23 | async-start | bytes 2621440 | tf_op jit(solution)/shard_map/reduce_scatter | solution.py:360
  1232.6 422.7 %reduce-scatter.20.cloned.1.call-start = ((), (), s32[]{:S(2)}) async-start(), calls=%async_computation.22 | async-start | bytes 2621440 | tf_op jit(solution)/shard_map/reduce_scatter | solution.py:359
  1237.8 451.7 %reduce-scatter.24.cloned.1.call-start = ((), (), s32[]{:S(2)}) async-start(), calls=%async_computation.24 | async-start | bytes 2621440 | tf_op jit(solution)/shard_map/reduce_scatter | solution.py:361
  (69 other events, 1229.6 us)
Sparse Core Ops, SparseCore 0:
  9.5 19.4 all-gather.9
  30.6 16.6 all-gather.7
  48.9 16.6 all-gather.11
  70.6 16.2 all-gather.13
  198.3 145.1 reduce-scatter.11
  344.9 33.5 all-gather.15
  380.0 34.4 all-gather.17
  416.1 34.4 all-gather.19
  524.4 145.3 reduce-scatter.13
  831.7 148.5 reduce-scatter.15
  1183.5 145.4 reduce-scatter.17
  1332.0 71.7 reduce-scatter.31
  1406.9 71.3 reduce-scatter.29
  1481.4 71.3 reduce-scatter.27
  1555.7 31.1 reduce-scatter.25
  1589.9 31.1 reduce-scatter.21
  1624.1 31.1 reduce-scatter.19
  1658.2 31.1 reduce-scatter.23
